TPU v7x, 32 devices: a whole 2x2x4 slice. The times are simulated.
32 devices in a mesh: section: 4 (over y, x), fsdp: 8 (over z, core).
Axes of the slice: x: 2, y: 2, z: 4, core: 2. Of those that a mesh axis runs over, the one named last changes fastest.
Arguments:
- grad_parts: bfloat16 [4, 8, 8192, 1024], P('section', 'fsdp'), may hold values from -510 to 510
- first_codes: int32 [4, 8192, 1024], P('section', 'fsdp'), may hold values from -7 to 7
- first_rows: float32 [4, 8192], P('section', 'fsdp'), may hold values from 0.003 to 0.03
- first_columns: float32 [4, 1024], P('section'), may hold values from 0.003 to 0.03
- second_codes: int32 [4, 8192, 1024], P('section', 'fsdp'), may hold values from 1 to 15
- second_rows: float32 [4, 8192], P('section', 'fsdp'), may hold values from 0.001 to 0.01
- second_columns: float32 [4, 1024], P('section'), may hold values from 0.001 to 0.01
Outputs:
- direction: float32 [4, 8192, 1024], P('section', 'fsdp')
- first_scaled: float32 [4, 8192, 1024], P('section', 'fsdp')
- second_scaled: float32 [4, 8192, 1024], P('section', 'fsdp')
- first_rowmax: float32 [4, 8192], P('section', 'fsdp')
- first_colmax: float32 [4, 1024], P('section')
- second_rowmax: float32 [4, 8192], P('section', 'fsdp')
- second_colmax: float32 [4, 1024], P('section')
All inputs are finite; a program needn't handle non-finite values. Where the computation divides by a largest or mean magnitude, that divisor is 1e-20 or more.
Results may differ from a plain program's by a relative error of at most 0.0003.
Values may be sent and summed in bfloat16 or wider, within the bound.
A program may use at most 192 MiB of HBM per device.

v0:
```python
import math

import jax
import jax.numpy as jnp
from jax import lax
from jax.sharding import PartitionSpec as P

beta_first = 0.9
beta_second = 0.999
clip_rms = 3.0
epsilon = 1e-08
scale_floor = 0.001


def dequantize(code_values, levels, row_scale, col_scale):
    scale_bound = jnp.minimum(row_scale[:, :, None], col_scale[:, None, :])
    return code_values.astype(jnp.float32) / levels * scale_bound


def moments(
    gradient,
    clip_scale,
    first_codes,
    first_rows,
    first_columns,
    second_codes,
    second_rows,
    second_columns,
):
    first_old = dequantize(first_codes, 7.0, first_rows, first_columns)
    second_old = dequantize(second_codes, 15.0, second_rows, second_columns)
    clipped = clip_scale * gradient
    first_new = beta_first * first_old + (1.0 - beta_first) * clipped
    second_new = beta_second * second_old + (1.0 - beta_second) * clipped * clipped
    direction = first_new / (jnp.sqrt(second_new) + epsilon)
    return (first_new, second_new, direction)


def local(
    grad_parts, first_codes, first_rows, first_columns, second_codes, second_rows, second_columns
):
    layer_count = grad_parts.shape[0]
    row_count = grad_parts.shape[2]
    col_count = grad_parts.shape[3]
    entries = layer_count * lax.axis_size("section") * row_count * col_count
    summands = grad_parts.reshape(layer_count, row_count, col_count).astype(jnp.float32)
    gradient = lax.psum_scatter(summands, "fsdp", scatter_dimension=1, tiled=True)
    square_sum = lax.psum(jnp.sum(gradient * gradient), ("section", "fsdp"))
    clip_limit = clip_rms * math.sqrt(entries)
    clip_scale = clip_limit / jnp.maximum(jnp.sqrt(square_sum), clip_limit)
    first_new, second_new, direction = moments(
        gradient,
        clip_scale,
        first_codes,
        first_rows,
        first_columns,
        second_codes,
        second_rows,
        second_columns,
    )
    first_rowmax = jnp.maximum(jnp.max(jnp.abs(first_new), axis=2), scale_floor)
    first_local = jnp.max(jnp.abs(first_new), axis=1)
    second_rowmax = jnp.max(second_new, axis=2)
    second_local = jnp.max(second_new, axis=1)
    first_colmax = lax.pmax(first_local, "fsdp")
    second_colmax = lax.pmax(second_local, "fsdp")
    first_colmax = jnp.maximum(first_colmax, scale_floor)
    first_scaled = first_new / jnp.minimum(first_rowmax[:, :, None], first_colmax[:, None, :])
    second_scaled = second_new / jnp.minimum(second_rowmax[:, :, None], second_colmax[:, None, :])
    return (
        direction,
        first_scaled,
        second_scaled,
        first_rowmax,
        first_colmax,
        second_rowmax,
        second_colmax,
    )


def solution(mesh):
    placed = (
        P("section", "fsdp", None, None),
        P("section", "fsdp", None),
        P("section", "fsdp"),
        P("section", None),
        P("section", "fsdp", None),
        P("section", "fsdp"),
        P("section", None),
    )
    return jax.shard_map(
        local,
        mesh=mesh,
        in_specs=placed,
        out_specs=(
            P("section", "fsdp", None),
            P("section", "fsdp", None),
            P("section", "fsdp", None),
            P("section", "fsdp"),
            P("section", None),
            P("section", "fsdp"),
            P("section", None),
        ),
        check_vma=False,
    )
```

profile of v0, /device:TPU:0, one launch (start us, length us, event | category | flops | bytes accessed | tf_op | source)
XLA Modules:
  0.0 435.0 jit_solution(17804462843008755610)
XLA Ops:
  7.2 0.0 reduce-scatter.2.cloned.1.call-start
  7.2 18.6 %bitcast_convert_fusion = f32[1,8192,1024]{2,1,0:T(8,128)} fusion(bf16[1,1,8192,1024]{3,2,1,0:T(8,128)(2,1)} %param.7), kind=kLoop, calls=%fused_computation | loop fusion | flops 8388608 | bytes 50331648 | tf_op jit(solution)/shard_map/convert_element_type | solution.py:46
  25.8 0.0 reduce-scatter.2.cloned.1.call-update
  25.8 0.0 copy-start.3
  25.8 0.0 copy-start.4
  25.8 0.0 copy-start.5
  25.9 0.0 copy-start.6
  25.9 328.3 %reduce-scatter.2.cloned.1.call-done = f32[1,1024,1024]{2,1,0:T(8,128)} async-done(((f32[1,8192,1024]{2,1,0:T(8,128)}), f32[1,1024,1024]{2,1,0:T(8,128)}) %reduce-scatter.2.cloned.1.call-update) | async-done | bytes 4194320 | tf_op jit(solution)/shard_map/reduce_scatter | solution.py:47
  354.2 3.9 multiply_reduce_fusion
  358.0 37.9 %psum.7 = f32[]{:T(128)} all-reduce(f32[]{:T(128)} %multiply_reduce_fusion), channel_id=1, replica_groups=mesh['section'=4,'fsdp'=8] {'section','fsdp'}, use_global_device_ids=true, to_apply=%region_2.0 | all-reduce | flops 1 | bytes 8 | tf_op jit(solution)/shard_map/psum | solution.py:48
  396.7 0.0 copy-done.3
  396.7 0.0 copy-done.4
  396.7 0.0 copy-done.5
  396.7 0.0 copy-done.6
  396.7 8.4 %fusion.1 = (f32[1024]{0:T(1024)S(1)}, f32[1024]{0:T(1024)S(1)}, f32[1,1024,1024]{2,1,0:T(8,128)}, f32[1024]{0:T(1024)S(1)}, f32[1024]{0:T(1024)S(1)}, /*index=5*/f32[1,1024,1024]{2,1,0:T(8,128)}) fusion(f32[1,1024,1024]{2,1,0:T(8,128)} %reduce-scatter.2.cloned.1.call-done, f32[]{:T(128)S(6)} %div.26, f32[1024]{0:T(1024)S(1)} %bitcast.18, ...), kind=kLoop, calls=%fused_computation.12 | loop fusion | flops 22016000 | bytes 21004292 | tf_op jit(solution)/shard_map/reduce_max | solution.py:63
  405.1 0.0 copy-start
  405.1 14.9 %all-reduce = (f32[1,1024]{1,0:T(1,128)S(1)}, f32[1,1024]{1,0:T(1,128)S(1)}) all-reduce(f32[1,1024]{1,0:T(1,128)S(1)} %bitcast.17, f32[1,1024]{1,0:T(1,128)S(1)} %bitcast.16), channel_id=1, replica_groups=mesh['section'=4,'fsdp'=8] {'fsdp'}, use_global_device_ids=true, to_apply=%region_5.0 | all-reduce | flops 2048 | bytes 16384 | tf_op jit(solution)/shard_map/pmax | solution.py:65
  420.0 0.0 copy-start.7
  420.1 0.0 copy-start.1
  420.1 0.0 copy-start.2
  420.1 8.1 %minimum_divide_fusion = (f32[1,1024,1024]{2,1,0:T(8,128)}, f32[1,1024,1024]{2,1,0:T(8,128)}, f32[1,1024,1024]{2,1,0:T(8,128)}) fusion(f32[1,1024,1024]{2,1,0:T(8,128)} %get-tuple-element.13, f32[1024]{0:T(1024)S(1)} %bitcast.22, f32[1024]{0:T(1024)S(1)} %get-tuple-element.7, f32[1,1024,1024]{2,1,0:T(8,128)} %get-tuple-element.20, f32[1024]{0:T(1024)S(1)} %bitcast.14, ...), kind=kLoop, calls=%fused_computation.3 | loop fusion | flops 6291456 | bytes 20987904 | tf_op jit(solution)/shard_map/div | solution.py:69
  428.2 0.0 copy-done
  428.2 0.0 copy-done.7
  428.2 0.0 copy-done.1
  428.2 0.0 copy-done.2
  (2 shorter events, 0.0 us)
Async XLA Ops:
  7.2 347.0 %reduce-scatter.2.cloned.1.call-start = ((), (), s32[]{:S(2)}) async-start(), calls=%async_computation.1 | async-start | bytes 37748736 | tf_op jit(solution)/shard_map/reduce_scatter | solution.py:47
  25.8 370.9 %copy-start.3 = (f32[1,1024]{1,0:T(1,128)S(1)}, f32[1,1024]{1,0:T(1,128)}, u32[]{:S(2)}) copy-start(f32[1,1024]{1,0:T(1,128)} %param.13) | copy-start | bytes 12292
  25.8 370.9 %copy-start.4 = (f32[1,1024]{1,0:T(1,128)S(1)}, f32[1,1024]{1,0:T(1,128)}, u32[]{:S(2)}) copy-start(f32[1,1024]{1,0:T(1,128)} %param.12) | copy-start | bytes 12292
  25.8 370.9 %copy-start.5 = (f32[1,1024]{1,0:T(1,128)S(1)}, f32[1,1024]{1,0:T(1,128)}, u32[]{:S(2)}) copy-start(f32[1,1024]{1,0:T(1,128)} %param.10) | copy-start | bytes 12292
  25.9 370.9 %copy-start.6 = (f32[1,1024]{1,0:T(1,128)S(1)}, f32[1,1024]{1,0:T(1,128)}, u32[]{:S(2)}) copy-start(f32[1,1024]{1,0:T(1,128)} %param.9) | copy-start | bytes 12292
  405.1 23.1 %copy-start = (f32[1024]{0:T(1024)}, f32[1024]{0:T(1024)S(1)}, u32[]{:S(2)}) copy-start(f32[1024]{0:T(1024)S(1)} %get-tuple-element.7) | copy-start | bytes 12292
  420.0 8.1 %copy-start.7 = (f32[1,1024]{1,0:T(1,128)}, f32[1,1024]{1,0:T(1,128)S(1)}, u32[]{:S(2)}) copy-start(f32[1,1024]{1,0:T(1,128)S(1)} %get-tuple-element.12) | copy-start | bytes 12292
  420.1 8.1 %copy-start.1 = (f32[1,1024]{1,0:T(1,128)}, f32[1,1024]{1,0:T(1,128)S(1)}, u32[]{:S(2)}) copy-start(f32[1,1024]{1,0:T(1,128)S(1)} %broadcast_maximum_fusion) | copy-start | bytes 12292
  420.1 8.1 %copy-start.2 = (f32[1024]{0:T(1024)}, f32[1024]{0:T(1024)S(1)}, u32[]{:S(2)}) copy-start(f32[1024]{0:T(1024)S(1)} %broadcast_maximum_fusion.1) | copy-start | bytes 12292
Sparse Core Ops, SparseCore 0:
  25.9 328.1 reduce-scatter.1
where the time goes:
time: 435 us
  waiting for transfers between devices  328 us (75%)
  blocking collectives  52.8 us (12%)
  other arithmetic  38.9 us (9%)
  between operations  14.9 us (3%)
    reduce_scatter x1, waiting for transfers between devices, local(): lax.psum_scatter(summands, 'fsdp', scatter_dimension=1, tiled=True)  328 us
    psum x1, blocking collectives, local(): square_sum = lax.psum(jnp.sum(gradient * gradient), ('section', 'fsdp'))  37.9 us
    convert_element_type x1, other arithmetic, local(): grad_parts.reshape(layer_count, row_count, col_count).astype(jnp.float32)  18.6 us
    pmax x1, blocking collectives, local(): first_colmax = lax.pmax(first_local, 'fsdp')  14.9 us
  transfers between devices with their start and end apart: 1, of which 1 were waited for; matrix products, arithmetic and copies ran while one was open for 0% of the time, Pallas kernels for 0%

commit v1 on v0

v1 whole, which is shorter than its diff:
```python
import functools
import math

import jax
import jax.numpy as jnp
from jax import lax
from jax.experimental import pallas as pl
from jax.experimental.pallas import tpu as pltpu
from jax.sharding import PartitionSpec as P

beta_first = 0.9
beta_second = 0.999
clip_rms = 3.0
epsilon = 1e-08
scale_floor = 0.001

CORES = 2
SLAB = 128
LANES = 128
VMEM_BYTES = 67043328
F32 = jnp.float32


def exchange_kernel(
    chips,
    fsdp,
    sections,
    slabs,
    clip_limit,
    grads,
    first_codes,
    first_rows,
    first_cols,
    second_codes,
    second_rows,
    second_cols,
    first_out,
    second_out,
    first_colmax,
    second_colmax,
    own,
    part,
    right_sum,
    left_sum,
    total,
    codes_a,
    codes_b,
    first,
    second,
    square_send,
    square_recv,
    cross_send,
    cross_recv,
    col_send,
    col_recv,
    own_sem,
    part_send_sem,
    part_recv_sem,
    right_send_sem,
    right_recv_sem,
    left_send_sem,
    left_recv_sem,
    code_sem,
    out_sem,
    square_sems,
    cross_sems,
    col_sems,
):
    me = lax.axis_index("fsdp")
    section = lax.axis_index("section")
    chip = me // CORES
    core = me % CORES
    partner = chip * CORES + (1 - core)
    right = ((chip + 1) % chips) * CORES + core
    left = ((chip + chips - 1) % chips) * CORES + core
    cols = total.shape[-1]
    items = (chips - 1) * slabs

    def own_copy(dest, slab):
        return pltpu.make_async_copy(
            grads.at[dest, core, slab], own.at[dest, slab], own_sem.at[dest * slabs + slab]
        )

    def part_copy(dest, slab):
        return pltpu.make_async_remote_copy(
            src_ref=grads.at[dest, 1 - core, slab],
            dst_ref=part.at[dest, slab],
            send_sem=part_send_sem.at[dest * slabs + slab],
            recv_sem=part_recv_sem.at[dest * slabs + slab],
            device_id={"fsdp": partner},
            device_id_type=pl.DeviceIdType.MESH,
        )

    def right_copy(dest, slab):
        slot = (dest - 1) * slabs + slab
        return pltpu.make_async_remote_copy(
            src_ref=right_sum.at[dest - 1, slab],
            dst_ref=right_sum.at[dest - 1, slab],
            send_sem=right_send_sem.at[slot],
            recv_sem=right_recv_sem.at[slot],
            device_id={"fsdp": right},
            device_id_type=pl.DeviceIdType.MESH,
        )

    def left_copy(dest, slab):
        slot = dest * slabs + slab
        return pltpu.make_async_remote_copy(
            src_ref=left_sum.at[dest, slab],
            dst_ref=left_sum.at[dest, slab],
            send_sem=left_send_sem.at[slot],
            recv_sem=left_recv_sem.at[slot],
            device_id={"fsdp": left},
            device_id_type=pl.DeviceIdType.MESH,
        )

    def wait_pair(dest, slab):
        own_copy(dest, slab).wait()
        part_copy(dest, slab).wait_recv()

    def pair_sum(dest, slab):
        return own[dest, slab].astype(F32) + part[dest, slab].astype(F32)

    @pl.loop(0, chips * slabs)
    def _(i):
        step, slab = i // slabs, i % slabs
        dest = jnp.where(2 * chip < chips, chips - 1 - step, step)
        own_copy(dest, slab).start()
        part_copy(dest, slab).start()

    code_copies = (
        pltpu.make_async_copy(first_codes, codes_a, code_sem.at[0]),
        pltpu.make_async_copy(second_codes, codes_b, code_sem.at[1]),
    )
    for copy in code_copies:
        copy.start()

    @pl.when(chip == 0)
    def _():
        @pl.loop(0, items)
        def _(j):
            dest, slab = chips - 1 - j // slabs, j % slabs
            wait_pair(dest, slab)
            right_sum[dest - 1, slab] = pair_sum(dest, slab)
            right_copy(dest, slab).start()

    @pl.when(chip == chips - 1)
    def _():
        @pl.loop(0, items)
        def _(j):
            dest, slab = j // slabs, j % slabs
            wait_pair(dest, slab)
            left_sum[dest, slab] = pair_sum(dest, slab)
            left_copy(dest, slab).start()

    @pl.loop(0, slabs)
    def _(slab):
        wait_pair(chip, slab)
        total[slab] = pair_sum(chip, slab)

    for copy in code_copies:
        copy.wait()

    @pl.loop(0, slabs)
    def _(slab):
        rows = pl.ds(pl.multiple_of(slab * SLAB, SLAB), SLAB)
        first_row = jnp.broadcast_to(first_rows[:, rows], (LANES, SLAB)).T
        second_row = jnp.broadcast_to(second_rows[:, rows], (LANES, SLAB)).T
        for q in range(cols // LANES):
            span = pl.ds(q * LANES, LANES)
            first_bound = jnp.minimum(first_row, first_cols[:, span])
            second_bound = jnp.minimum(second_row, second_cols[:, span])
            first_old = codes_a[slab, :, span].astype(F32) / 7.0 * first_bound
            second_old = codes_b[slab, :, span].astype(F32) / 15.0 * second_bound
            first[slab, :, span] = beta_first * first_old
            second[slab, :, span] = beta_second * second_old

    @pl.loop(0, items)
    def _(j):
        slab = j % slabs
        dest = chips - 1 - j // slabs

        @pl.when((chip > 0) & (dest > chip))
        def _():
            right_copy(dest, slab).wait_recv()
            wait_pair(dest, slab)
            right_sum[dest - 1, slab] += pair_sum(dest, slab)
            right_copy(dest, slab).start()

        @pl.when((chip > 0) & (dest == chip))
        def _():
            right_copy(dest, slab).wait_recv()
            total[slab] += right_sum[dest - 1, slab]

        low = j // slabs

        @pl.when((chip < chips - 1) & (low < chip))
        def _():
            left_copy(low, slab).wait_recv()
            wait_pair(low, slab)
            left_sum[low, slab] += pair_sum(low, slab)
            left_copy(low, slab).start()

        @pl.when((chip < chips - 1) & (low == chip))
        def _():
            left_copy(low, slab).wait_recv()
            total[slab] += left_sum[low, slab]

    piece = 16
    pieces = SLAB // piece

    def add_squares(i, acc):
        slab, rows = i // pieces, pl.ds(pl.multiple_of((i % pieces) * piece, piece), piece)
        g = total[slab, rows, :]
        return acc + jnp.sum((g * g).reshape(piece // 8, 8, cols), axis=0)

    squares = lax.fori_loop(0, slabs * pieces, add_squares, jnp.zeros((8, cols), F32))
    folded = squares[:, :LANES]
    for q in range(1, cols // LANES):
        folded = folded + squares[:, q * LANES : (q + 1) * LANES]

    def to_all(axis, size, position, source, slots, sems):
        copies = [
            pltpu.make_async_remote_copy(
                src_ref=source,
                dst_ref=slots.at[s - 1],
                send_sem=sems.at[0, s - 1],
                recv_sem=sems.at[1, s - 1],
                device_id={axis: (position + s) % size},
                device_id_type=pl.DeviceIdType.MESH,
            )
            for s in range(1, size)
        ]
        for copy in copies:
            copy.start()
        return copies

    square_send[...] = folded
    square_copies = to_all("fsdp", fsdp, me, square_send, square_recv, square_sems)
    for s, copy in enumerate(square_copies):
        copy.wait_recv()
        folded = folded + square_recv[s]
    cross_send[...] = folded
    cross_copies = to_all("section", sections, section, cross_send, cross_recv, cross_sems)
    for s, copy in enumerate(cross_copies):
        copy.wait_recv()
        folded = folded + cross_recv[s]
    square_sum = jnp.sum(jnp.sum(folded, axis=0, keepdims=True), axis=1, keepdims=True)
    norm = jnp.sqrt(jnp.broadcast_to(square_sum, (1, cols)))
    scale = clip_limit / jnp.maximum(norm, clip_limit)

    def out_copies(slab):
        return (
            pltpu.make_async_copy(first.at[slab], first_out.at[slab], out_sem.at[0, slab]),
            pltpu.make_async_copy(second.at[slab], second_out.at[slab], out_sem.at[1, slab]),
        )

    def update_slab(slab, carry):
        def update_piece(i, carry):
            first_top, second_top = carry
            rows = pl.ds(pl.multiple_of(i * piece, piece), piece)
            clipped = scale * total[slab, rows, :]
            first_new = first[slab, rows, :] + (1.0 - beta_first) * clipped
            second_new = second[slab, rows, :] + (1.0 - beta_second) * clipped * clipped
            first[slab, rows, :] = first_new
            second[slab, rows, :] = second_new
            high = jnp.max(jnp.abs(first_new).reshape(piece // 8, 8, cols), axis=0)
            top = jnp.max(second_new.reshape(piece // 8, 8, cols), axis=0)
            return jnp.maximum(first_top, high), jnp.maximum(second_top, top)

        carry = lax.fori_loop(0, pieces, update_piece, carry)
        for copy in out_copies(slab):
            copy.start()
        return carry

    nothing = jnp.zeros((8, cols), F32)
    first_top, second_top = lax.fori_loop(0, slabs, update_slab, (nothing, nothing))
    first_top = jnp.max(first_top, axis=0, keepdims=True)
    second_top = jnp.max(second_top, axis=0, keepdims=True)
    col_send[0:1, :] = first_top
    col_send[1:2, :] = second_top
    col_copies = to_all("fsdp", fsdp, me, col_send, col_recv, col_sems)

    @pl.loop(0, chips * slabs)
    def _(i):
        part_copy(i // slabs, i % slabs).wait_send()

    @pl.loop(0, items)
    def _(j):
        slab = j % slabs

        @pl.when(j // slabs + 1 > chip)
        def _():
            right_copy(j // slabs + 1, slab).wait_send()

        @pl.when(j // slabs < chip)
        def _():
            left_copy(j // slabs, slab).wait_send()

    for copy in square_copies + cross_copies:
        copy.wait_send()

    for s, copy in enumerate(col_copies):
        copy.wait_recv()
        first_top = jnp.maximum(first_top, col_recv[s, 0:1, :])
        second_top = jnp.maximum(second_top, col_recv[s, 1:2, :])
    first_colmax[...] = jnp.maximum(first_top, scale_floor)
    second_colmax[...] = second_top
    for copy in col_copies:
        copy.wait_send()

    @pl.loop(0, slabs)
    def _(slab):
        for copy in out_copies(slab):
            copy.wait()


def finish_kernel(
    first,
    second,
    first_colmax,
    second_colmax,
    direction,
    first_scaled,
    second_scaled,
    first_rowmax,
    second_rowmax,
):
    first_new = first[0]
    second_new = second[0]
    first_top = jnp.maximum(jnp.max(jnp.abs(first_new), axis=1, keepdims=True), scale_floor)
    second_top = jnp.max(second_new, axis=1, keepdims=True)
    direction[0] = first_new / (jnp.sqrt(second_new) + epsilon)
    first_scaled[0] = first_new / jnp.minimum(first_top, first_colmax[...])
    second_scaled[0] = second_new / jnp.minimum(second_top, second_colmax[...])
    first_rowmax[...] = jnp.broadcast_to(first_top, (SLAB, LANES)).T[0:1, :]
    second_rowmax[...] = jnp.broadcast_to(second_top, (SLAB, LANES)).T[0:1, :]


def local(
    grad_parts, first_codes, first_rows, first_columns, second_codes, second_rows, second_columns
):
    fsdp = lax.axis_size("fsdp")
    sections = lax.axis_size("section")
    layers, _, row_count, cols = grad_parts.shape
    chips = fsdp // CORES
    rows = row_count // fsdp
    slabs = rows // SLAB
    clip_limit = clip_rms * math.sqrt(layers * sections * row_count * cols)
    grads = grad_parts.reshape(chips, CORES, slabs, SLAB, cols)
    tiled = (slabs, SLAB, cols)
    items = (chips - 1) * slabs
    hbm = pl.BlockSpec(memory_space=pl.ANY)
    vmem = pl.BlockSpec(memory_space=pltpu.VMEM)
    dma = pltpu.SemaphoreType.DMA
    first_new, second_new, first_colmax, second_colmax = pl.pallas_call(
        functools.partial(exchange_kernel, chips, fsdp, sections, slabs, clip_limit),
        out_shape=(
            jax.ShapeDtypeStruct(tiled, F32),
            jax.ShapeDtypeStruct(tiled, F32),
            jax.ShapeDtypeStruct((1, cols), F32),
            jax.ShapeDtypeStruct((1, cols), F32),
        ),
        in_specs=[hbm, hbm, vmem, vmem, hbm, vmem, vmem],
        out_specs=(hbm, hbm, vmem, vmem),
        scratch_shapes=[
            pltpu.VMEM((chips, *tiled), jnp.bfloat16),
            pltpu.VMEM((chips, *tiled), jnp.bfloat16),
            pltpu.VMEM((chips - 1, *tiled), F32),
            pltpu.VMEM((chips - 1, *tiled), F32),
            pltpu.VMEM(tiled, F32),
            pltpu.VMEM(tiled, jnp.int32),
            pltpu.VMEM(tiled, jnp.int32),
            pltpu.VMEM(tiled, F32),
            pltpu.VMEM(tiled, F32),
            pltpu.VMEM((8, LANES), F32),
            pltpu.VMEM((fsdp - 1, 8, LANES), F32),
            pltpu.VMEM((8, LANES), F32),
            pltpu.VMEM((max(sections - 1, 1), 8, LANES), F32),
            pltpu.VMEM((2, cols), F32),
            pltpu.VMEM((fsdp - 1, 2, cols), F32),
            dma((chips * slabs,)),
            dma((chips * slabs,)),
            dma((chips * slabs,)),
            dma((items,)),
            dma((items,)),
            dma((items,)),
            dma((items,)),
            dma((2,)),
            dma((2, slabs)),
            dma((2, fsdp - 1)),
            dma((2, max(sections - 1, 1))),
            dma((2, fsdp - 1)),
        ],
        compiler_params=pltpu.CompilerParams(
            has_side_effects=True, vmem_limit_bytes=VMEM_BYTES
        ),
    )(
        grads,
        first_codes.reshape(tiled),
        first_rows,
        first_columns,
        second_codes.reshape(tiled),
        second_rows,
        second_columns,
    )
    block = pl.BlockSpec((1, SLAB, cols), lambda i: (i, 0, 0))
    whole = pl.BlockSpec((1, cols), lambda i: (0, 0))
    strip = pl.BlockSpec((1, SLAB), lambda i: (0, i))
    direction, first_scaled, second_scaled, first_rowmax, second_rowmax = pl.pallas_call(
        finish_kernel,
        grid=(slabs,),
        out_shape=(
            jax.ShapeDtypeStruct(tiled, F32),
            jax.ShapeDtypeStruct(tiled, F32),
            jax.ShapeDtypeStruct(tiled, F32),
            jax.ShapeDtypeStruct((1, rows), F32),
            jax.ShapeDtypeStruct((1, rows), F32),
        ),
        in_specs=[block, block, whole, whole],
        out_specs=(block, block, block, strip, strip),
    )(first_new, second_new, first_colmax, second_colmax)
    shape = (layers, rows, cols)
    return (
        direction.reshape(shape),
        first_scaled.reshape(shape),
        second_scaled.reshape(shape),
        first_rowmax,
        first_colmax,
        second_rowmax,
        second_colmax,
    )


def solution(mesh):
    placed = (
        P("section", "fsdp", None, None),
        P("section", "fsdp", None),
        P("section", "fsdp"),
        P("section", None),
        P("section", "fsdp", None),
        P("section", "fsdp"),
        P("section", None),
    )
    return jax.shard_map(
        local,
        mesh=mesh,
        in_specs=placed,
        out_specs=(
            P("section", "fsdp", None),
            P("section", "fsdp", None),
            P("section", "fsdp", None),
            P("section", "fsdp"),
            P("section", None),
            P("section", "fsdp"),
            P("section", None),
        ),
        check_vma=False,
    )
```

time: 435 us -> 387 us (0.89)
  Pallas kernels: 0 us -> 385 us
  waiting for transfers between devices: 328 us -> 0 us
  blocking collectives: 52.8 us -> 0 us
  other arithmetic: 38.9 us -> 0 us
  between operations: 14.9 us -> 0.66 us
    pallas_call x0 -> x2, Pallas kernels: none -> 385 us  [the longest x1 374 us: local(): pl.pallas_call(functools.partial(exchange_kernel, chips, fsdp, sections,...]
    reduce_scatter x1 -> x0, waiting for transfers between devices: 328 us -> none  [local(): lax.psum_scatter(summands, 'fsdp', scatter_dimension=1, tiled=True)]
    psum x1 -> x0, blocking collectives: 37.9 us -> none  [local(): square_sum = lax.psum(jnp.sum(gradient * gradient), ('section', 'fsdp'))]
    convert_element_type x1 -> x0, other arithmetic: 18.6 us -> none  [local(): grad_parts.reshape(layer_count, row_count, col_count).astype(jnp.float32)]
    pmax x1 -> x0, blocking collectives: 14.9 us -> none  [local(): first_colmax = lax.pmax(first_local, 'fsdp')]
    reduce_max x1 -> x0, other arithmetic: 8.36 us -> none  [local(): second_rowmax = jnp.max(second_new, axis=2)]
    div x1 -> x0, other arithmetic: 8.06 us -> none  [local(): second_new / jnp.minimum(second_rowmax[:, :, None], second_colmax[:, None...]
  transfers between devices with their start and end apart: 1 -> 0, of which waited for: 1 -> 0; matrix products, arithmetic and copies ran while one was open for 0% -> 0% of each run, Pallas kernels for 0% -> 0%
where the time goes in v1:
time: 387 us; the launch traced here: 386 us
  Pallas kernels  385 us (99%)
    pallas_call x1, Pallas kernels, local(): pl.pallas_call(functools.partial(exchange_kernel, chips, fsdp, sections,...  374 us
    pallas_call x1, Pallas kernels, local(): pl.pallas_call(finish_kernel, grid=(slabs,), out_shape=(jax.ShapeDtypeStr...  10.5 us

profile of v1, /device:TPU:0, one launch (start us, length us, event | category | flops | bytes accessed | tf_op | source)
XLA Modules:
  0.0 386.5 jit_solution(5417391541145910861)
XLA Ops:
  0.6 374.1 %shard_map.126 = (f32[8,128,1024]{2,1,0:T(8,128)}, f32[8,128,1024]{2,1,0:T(8,128)}, f32[1,1024]{1,0:T(1,128)}, f32[1,1024]{1,0:T(1,128)}) custom-call(bf16[4,2,8,128,1024]{4,3,2,1,0:T(8,128)(2,1)} %bitcast.6, s32[8,128,1024]{2,1,0:T(8,128)} %bitcast.7, f32[1,1024]{1,0:T(1,128)} %first_rows.1, f32[1,1024]{1,0:T(1,128)} %first_cols.1, ...), custom_call_target="tpu_custom_call" | custom-call | tf_op jit(solution)/shard_map/pallas_call | solution.py:355
  374.7 0.0 copy-start.1
  374.7 0.0 copy-start
  374.7 10.5 %shard_map.127 = (f32[8,128,1024]{2,1,0:T(8,128)}, f32[8,128,1024]{2,1,0:T(8,128)}, f32[8,128,1024]{2,1,0:T(8,128)}, f32[1,1024]{1,0:T(1,128)}, f32[1,1024]{1,0:T(1,128)}) custom-call(f32[8,128,1024]{2,1,0:T(8,128)} %get-tuple-element.16.first, f32[8,128,1024]{2,1,0:T(8,128)} %get-tuple-element.17.second, f32[1,1024]{1,0:T(1,128)} %get-tuple-element.36.first_colmax, ...), custom_call_target="tpu_custom_call" | custom-call | tf_op jit(solution)/shard_map/pallas_call | solution.py:409
  385.3 0.0 copy-done.1
  385.3 0.6 copy.16
  385.9 0.0 copy-done
  385.9 0.6 copy.17
Async XLA Ops:
  374.7 10.6 %copy-start.1 = (f32[1,1024]{1,0:T(1,128)S(1)}, f32[1,1024]{1,0:T(1,128)}, u32[]{:S(2)}) copy-start(f32[1,1024]{1,0:T(1,128)} %get-tuple-element.36.first_colmax) | copy-start | bytes 12292
  374.7 11.2 %copy-start = (f32[1,1024]{1,0:T(1,128)S(1)}, f32[1,1024]{1,0:T(1,128)}, u32[]{:S(2)}) copy-start(f32[1,1024]{1,0:T(1,128)} %get-tuple-element.38.second_colmax) | copy-start | bytes 12292

commit v2 on v1

--- a/solution.py
+++ b/solution.py
@@ -17,6 +17,7 @@
 CORES = 2
 SLAB = 128
 LANES = 128
+LAG = 2
 VMEM_BYTES = 67043328
 F32 = jnp.float32
 
@@ -174,36 +175,42 @@
             first[slab, :, span] = beta_first * first_old
             second[slab, :, span] = beta_second * second_old
 
-    @pl.loop(0, items)
-    def _(j):
+    right_lag = LAG * chip
+    left_lag = LAG * (chips - 1 - chip)
+
+    @pl.loop(0, items + LAG * (chips - 1))
+    def _(step):
+        j = step - right_lag
+        dest = chips - 1 - j // slabs
         slab = j % slabs
-        dest = chips - 1 - j // slabs
-
-        @pl.when((chip > 0) & (dest > chip))
+
+        @pl.when((chip > 0) & (j >= 0) & (dest > chip))
         def _():
             right_copy(dest, slab).wait_recv()
             wait_pair(dest, slab)
             right_sum[dest - 1, slab] += pair_sum(dest, slab)
             right_copy(dest, slab).start()
 
-        @pl.when((chip > 0) & (dest == chip))
+        @pl.when((chip > 0) & (j >= 0) & (dest == chip))
         def _():
             right_copy(dest, slab).wait_recv()
             total[slab] += right_sum[dest - 1, slab]
 
-        low = j // slabs
-
-        @pl.when((chip < chips - 1) & (low < chip))
-        def _():
-            left_copy(low, slab).wait_recv()
-            wait_pair(low, slab)
-            left_sum[low, slab] += pair_sum(low, slab)
-            left_copy(low, slab).start()
-
-        @pl.when((chip < chips - 1) & (low == chip))
-        def _():
-            left_copy(low, slab).wait_recv()
-            total[slab] += left_sum[low, slab]
+        i = step - left_lag
+        low = i // slabs
+        strip = i % slabs
+
+        @pl.when((chip < chips - 1) & (i >= 0) & (low < chip))
+        def _():
+            left_copy(low, strip).wait_recv()
+            wait_pair(low, strip)
+            left_sum[low, strip] += pair_sum(low, strip)
+            left_copy(low, strip).start()
+
+        @pl.when((chip < chips - 1) & (i >= 0) & (low == chip))
+        def _():
+            left_copy(low, strip).wait_recv()
+            total[strip] += left_sum[low, strip]
 
     piece = 16
     pieces = SLAB // piece
@@ -324,6 +331,8 @@
     second_scaled,
     first_rowmax,
     second_rowmax,
+    first_kept,
+    second_kept,
 ):
     first_new = first[0]
     second_new = second[0]
@@ -334,6 +343,8 @@
     second_scaled[0] = second_new / jnp.minimum(second_top, second_colmax[...])
     first_rowmax[...] = jnp.broadcast_to(first_top, (SLAB, LANES)).T[0:1, :]
     second_rowmax[...] = jnp.broadcast_to(second_top, (SLAB, LANES)).T[0:1, :]
+    first_kept[...] = first_colmax[...]
+    second_kept[...] = second_colmax[...]
 
 
 def local(
@@ -406,7 +417,7 @@
     block = pl.BlockSpec((1, SLAB, cols), lambda i: (i, 0, 0))
     whole = pl.BlockSpec((1, cols), lambda i: (0, 0))
     strip = pl.BlockSpec((1, SLAB), lambda i: (0, i))
-    direction, first_scaled, second_scaled, first_rowmax, second_rowmax = pl.pallas_call(
+    finished = pl.pallas_call(
         finish_kernel,
         grid=(slabs,),
         out_shape=(
@@ -415,10 +426,14 @@
             jax.ShapeDtypeStruct(tiled, F32),
             jax.ShapeDtypeStruct((1, rows), F32),
             jax.ShapeDtypeStruct((1, rows), F32),
+            jax.ShapeDtypeStruct((1, cols), F32),
+            jax.ShapeDtypeStruct((1, cols), F32),
         ),
         in_specs=[block, block, whole, whole],
-        out_specs=(block, block, block, strip, strip),
+        out_specs=(block, block, block, strip, strip, whole, whole),
     )(first_new, second_new, first_colmax, second_colmax)
+    direction, first_scaled, second_scaled = finished[:3]
+    first_rowmax, second_rowmax, first_colmax, second_colmax = finished[3:]
     shape = (layers, rows, cols)
     return (
         direction.reshape(shape),

time: 387 us -> 311 us (0.80)
  Pallas kernels: 385 us -> 310 us
    pallas_call x1, Pallas kernels: 374 us -> 299 us  [local(): pl.pallas_call(functools.partial(exchange_kernel, chips, fsdp, sections,...]
where the time goes in v2:
time: 311 us; the launch traced here: 310 us
  Pallas kernels  310 us (100%)
    pallas_call x1, Pallas kernels, local(): pl.pallas_call(functools.partial(exchange_kernel, chips, fsdp, sections,...  299 us
    pallas_call x1, Pallas kernels, local(): pl.pallas_call(finish_kernel, grid=(slabs,), out_shape=(jax.ShapeDtypeStr...  10.4 us

profile of v2, /device:TPU:0, one launch (start us, length us, event | category | flops | bytes accessed | tf_op | source)
XLA Modules:
  0.0 310.5 jit_solution(17252369706925334506)
XLA Ops:
  0.6 299.4 %shard_map.126 = (f32[8,128,1024]{2,1,0:T(8,128)}, f32[8,128,1024]{2,1,0:T(8,128)}, f32[1,1024]{1,0:T(1,128)}, f32[1,1024]{1,0:T(1,128)}) custom-call(bf16[4,2,8,128,1024]{4,3,2,1,0:T(8,128)(2,1)} %bitcast.6, s32[8,128,1024]{2,1,0:T(8,128)} %bitcast.7, f32[1,1024]{1,0:T(1,128)} %first_rows.1, f32[1,1024]{1,0:T(1,128)} %first_cols.1, ...), custom_call_target="tpu_custom_call" | custom-call | tf_op jit(solution)/shard_map/pallas_call | solution.py:366
  300.0 10.4 %shard_map.127 = (f32[8,128,1024]{2,1,0:T(8,128)}, f32[8,128,1024]{2,1,0:T(8,128)}, f32[8,128,1024]{2,1,0:T(8,128)}, f32[1,1024]{1,0:T(1,128)}, f32[1,1024]{1,0:...) custom-call(f32[8,128,1024]{2,1,0:T(8,128)} %get-tuple-element.18.first, f32[8,128,1024]{2,1,0:T(8,128)} %get-tuple-element.19.second, ...), custom_call_target="tpu_custom_call" | custom-call | tf_op jit(solution)/shard_map/pallas_call | solution.py:420
